TPU v7x, 32 devices: a whole 2x2x4 slice. The times are simulated.
32 devices in a mesh: replica: 2 (over x), data2: 4 (over z), data: 4 (over y, core).
Axes of the slice: x: 2, y: 2, z: 4, core: 2. Of those that a mesh axis runs over, the one named last changes fastest.
Arguments:
- q_hidden: bfloat16 [256, 32, 2048], P(('replica', 'data2', 'data')), parts along dimension 0
- d_hidden: bfloat16 [256, 768, 2048], P(('replica', 'data2', 'data')), parts along dimension 0
- w_proj: bfloat16 [2048, 128], replicated
- q_mask: int32 [256, 32], P(('replica', 'data2', 'data')), parts along dimension 0
- d_mask: int32 [256, 768], P(('replica', 'data2', 'data')), parts along dimension 0
- temperature: float32 [], replicated
Outputs:
- output 1: float32 [256], P(('replica', 'data2', 'data')), parts along dimension 0
- output 2: float32 [2], P('replica'), parts along dimension 0
There are 2 independent parts. A program takes and returns all parts, laid end to end along the dimension named above; an argument that names none is the same for every part.
All inputs are finite; a program needn't handle non-finite values.
Results may differ from a plain program's by a relative error of at most 0.00218619.
Values are sent between devices in bfloat16 or wider.
A program may use at most 1 GiB of HBM per device.

v0:
```python
import jax
import jax.numpy as jnp
from jax import lax
from jax.sharding import PartitionSpec as P

NORM_EPS = 1e-6
GROUP_AXES = ('data2', 'data')
ROW_AXES = ('replica', 'data2', 'data')


def project(hidden, w_proj):
    proj_f32 = jnp.einsum('bld,de->ble', hidden, w_proj, preferred_element_type=jnp.float32)
    row_norm = jnp.sqrt(jnp.sum(proj_f32 * proj_f32, axis=-1, keepdims=True) + NORM_EPS)
    return (proj_f32 / row_norm).astype(jnp.bfloat16)


def block_scores(q_block, d_tok, d_valid):
    sim_vals = jnp.einsum('qtd,psd->qtps', q_block, d_tok, preferred_element_type=jnp.float32)
    sim_vals = jnp.where(d_valid[None, None], sim_vals, -jnp.inf)
    return jnp.sum(jnp.max(sim_vals, axis=-1), axis=1)


def row_losses(row_scores, value_a11, my_index, per_dev):
    logits = row_scores / value_a11
    row_max = jnp.max(logits, axis=1, keepdims=True)
    log_norm = row_max[:, 0] + jnp.log(jnp.sum(jnp.exp(logits - row_max), axis=1))
    pos_tile = lax.dynamic_slice_in_dim(logits, my_index * per_dev, per_dev, axis=1)
    return log_norm - jnp.diagonal(pos_tile)


def solution(mesh):
    outer_size = mesh.shape['data2']
    inner_size = mesh.shape['data']
    group_size = outer_size * inner_size

    def device_fn(q_hidden, d_hidden, w_proj, q_mask, d_mask, value_a11):
        per_dev, q_len = q_mask.shape
        proj_dim = w_proj.shape[1]
        q_tok = jnp.where(q_mask[:, :, None] > 0, project(q_hidden, w_proj), jnp.zeros((), jnp.bfloat16))
        d_tok = project(d_hidden, w_proj)
        d_valid = d_mask > 0
        all_q = lax.all_gather(q_tok, GROUP_AXES, axis=0, tiled=True)
        all_q = all_q.reshape(group_size, per_dev, q_len, proj_dim)

        def score_block(q_block):
            return block_scores(q_block, d_tok, d_valid)

        col_scores = lax.map(score_block, all_q).reshape(outer_size, inner_size, per_dev, per_dev)
        col_scores = lax.all_to_all(col_scores, 'data', 1, 1, tiled=True)
        col_scores = lax.all_to_all(col_scores, 'data2', 0, 0, tiled=True)
        row_scores = jnp.transpose(col_scores, (2, 0, 1, 3)).reshape(per_dev, group_size * per_dev)
        my_index = lax.axis_index('data2') * inner_size + lax.axis_index('data')
        loss_rows = row_losses(row_scores, value_a11, my_index, per_dev)
        loss_mean = lax.psum(jnp.sum(loss_rows), GROUP_AXES) / (group_size * per_dev)
        return loss_rows, loss_mean.reshape(1)

    return jax.shard_map(
        device_fn,
        mesh=mesh,
        in_specs=(P(ROW_AXES), P(ROW_AXES), P(), P(ROW_AXES), P(ROW_AXES), P()),
        out_specs=(P(ROW_AXES), P('replica')),
        check_vma=False,
    )
```

profile of v0, /device:TPU:0, one launch (start us, length us, event | category | flops | bytes accessed | tf_op | source)
XLA Modules:
  0.0 153.1 jit_solution(2243978717646683314)
XLA Ops:
  11.5 14.4 %multiply_reduce_fusion = (f32[8,768]{1,0:T(8,128)S(1)}, f32[8,768,128]{1,2,0:T(8,128)}) fusion(bf16[8,768,2048]{2,1,0:T(8,128)(2,1)} %param.9, bf16[2048,128]{1,0:T(8,128)(2,1)} %param.10), kind=kOutput, calls=%fused_computation.8 | convolution fusion | flops 3222792192 | bytes 28860416 | tf_op jit(solution)/shard_map/bld,de->ble/dot_general | solution.py:12
  25.9 2.2 %divide_convert_fusion = bf16[8,768,128]{1,2,0:T(8,128)(2,1)S(1)} fusion(f32[8,768,128]{1,2,0:T(8,128)} %get-tuple-element.67, f32[8,768]{1,0:T(8,128)S(1)} %add_sqrt_fusion), kind=kLoop, calls=%fused_computation.7 | loop fusion | flops 1572864 | bytes 4743168 | tf_op jit(solution)/shard_map/convert_element_type | solution.py:14
  29.6 22.7 %all-gather.2.cloned.1.call-done = bf16[128,32,128]{2,1,0:T(8,128)(2,1)} async-done(((bf16[8,32,128]{2,1,0:T(8,128)(2,1)}), bf16[128,32,128]{2,1,0:T(8,128)(2,1)}) %all-gather.2.cloned.1.call-update) | async-done | bytes 1048592 | tf_op jit(solution)/shard_map/all_gather | solution.py:42
  52.3 41.7 %while.10 = (s32[]{:T(128)}, f32[16,8,8]{2,1,0:T(8,128)S(1)}, pred[8,768]{1,0:T(8,128)(4,1)S(1)}, bf16[16,8,32,128]{3,2,1,0:T(8,128)(2,1)}, bf16[8,768,128]{2,1,0:T(8,128)(2,1)}, /*index=5*/s32[]{:T(128)}, f32[]{:T(128)}) while((s32[]{:T(128)}, f32[16,8,8]{2,1,0:T(8,128)S(1)}, pred[8,768]{1,0:T(8,128)(4,1)S(1)}, ...), condition=%wide.region_5.6_spmd, body=%wide.region_2.5_spmd.sunk | while | flops 405798848 | bytes 1669973 | solution.py:48
  52.3 2.5 %select_reduce_fusion.2 = f32[8,32,8]{1,2,0:T(8,128)S(1)} fusion(pred[8,768]{1,0:T(8,128)(4,1)S(1)} %get-tuple-element.115, bf16[8,768,128]{2,1,0:T(8,128)(2,1)} %get-tuple-element.117, bf16[16,8,32,128]{3,2,1,0:T(8,128)(2,1)} %get-tuple-element.116, s32[]{:T(128)} %get-tuple-element.106), kind=kOutput, calls=%fused_computation.1.clone.1 | convolution fusion | flops 405796864 | bytes 1653248 | tf_op jit(solution)/shard_map/while/body/eval_jaxpr/qtd,psd->qtps/dot_general | solution.py:18
  54.9 2.5 %select_reduce_fusion.2 = f32[8,32,8]{1,2,0:T(8,128)S(1)} fusion(pred[8,768]{1,0:T(8,128)(4,1)S(1)} %get-tuple-element.115, bf16[8,768,128]{2,1,0:T(8,128)(2,1)} %get-tuple-element.117, bf16[16,8,32,128]{3,2,1,0:T(8,128)(2,1)} %get-tuple-element.116, s32[]{:T(128)} %get-tuple-element.106), kind=kOutput, calls=%fused_computation.1.clone.1 | convolution fusion | flops 405796864 | bytes 1653248 | tf_op jit(solution)/shard_map/while/body/eval_jaxpr/qtd,psd->qtps/dot_general | solution.py:18
  57.5 2.5 %select_reduce_fusion.2 = f32[8,32,8]{1,2,0:T(8,128)S(1)} fusion(pred[8,768]{1,0:T(8,128)(4,1)S(1)} %get-tuple-element.115, bf16[8,768,128]{2,1,0:T(8,128)(2,1)} %get-tuple-element.117, bf16[16,8,32,128]{3,2,1,0:T(8,128)(2,1)} %get-tuple-element.116, s32[]{:T(128)} %get-tuple-element.106), kind=kOutput, calls=%fused_computation.1.clone.1 | convolution fusion | flops 405796864 | bytes 1653248 | tf_op jit(solution)/shard_map/while/body/eval_jaxpr/qtd,psd->qtps/dot_general | solution.py:18
  60.1 2.5 %select_reduce_fusion.2 = f32[8,32,8]{1,2,0:T(8,128)S(1)} fusion(pred[8,768]{1,0:T(8,128)(4,1)S(1)} %get-tuple-element.115, bf16[8,768,128]{2,1,0:T(8,128)(2,1)} %get-tuple-element.117, bf16[16,8,32,128]{3,2,1,0:T(8,128)(2,1)} %get-tuple-element.116, s32[]{:T(128)} %get-tuple-element.106), kind=kOutput, calls=%fused_computation.1.clone.1 | convolution fusion | flops 405796864 | bytes 1653248 | tf_op jit(solution)/shard_map/while/body/eval_jaxpr/qtd,psd->qtps/dot_general | solution.py:18
  62.7 2.5 %select_reduce_fusion.2 = f32[8,32,8]{1,2,0:T(8,128)S(1)} fusion(pred[8,768]{1,0:T(8,128)(4,1)S(1)} %get-tuple-element.115, bf16[8,768,128]{2,1,0:T(8,128)(2,1)} %get-tuple-element.117, bf16[16,8,32,128]{3,2,1,0:T(8,128)(2,1)} %get-tuple-element.116, s32[]{:T(128)} %get-tuple-element.106), kind=kOutput, calls=%fused_computation.1.clone.1 | convolution fusion | flops 405796864 | bytes 1653248 | tf_op jit(solution)/shard_map/while/body/eval_jaxpr/qtd,psd->qtps/dot_general | solution.py:18
  65.3 2.5 %select_reduce_fusion.2 = f32[8,32,8]{1,2,0:T(8,128)S(1)} fusion(pred[8,768]{1,0:T(8,128)(4,1)S(1)} %get-tuple-element.115, bf16[8,768,128]{2,1,0:T(8,128)(2,1)} %get-tuple-element.117, bf16[16,8,32,128]{3,2,1,0:T(8,128)(2,1)} %get-tuple-element.116, s32[]{:T(128)} %get-tuple-element.106), kind=kOutput, calls=%fused_computation.1.clone.1 | convolution fusion | flops 405796864 | bytes 1653248 | tf_op jit(solution)/shard_map/while/body/eval_jaxpr/qtd,psd->qtps/dot_general | solution.py:18
  67.9 2.5 %select_reduce_fusion.2 = f32[8,32,8]{1,2,0:T(8,128)S(1)} fusion(pred[8,768]{1,0:T(8,128)(4,1)S(1)} %get-tuple-element.115, bf16[8,768,128]{2,1,0:T(8,128)(2,1)} %get-tuple-element.117, bf16[16,8,32,128]{3,2,1,0:T(8,128)(2,1)} %get-tuple-element.116, s32[]{:T(128)} %get-tuple-element.106), kind=kOutput, calls=%fused_computation.1.clone.1 | convolution fusion | flops 405796864 | bytes 1653248 | tf_op jit(solution)/shard_map/while/body/eval_jaxpr/qtd,psd->qtps/dot_general | solution.py:18
  70.5 2.5 %select_reduce_fusion.2 = f32[8,32,8]{1,2,0:T(8,128)S(1)} fusion(pred[8,768]{1,0:T(8,128)(4,1)S(1)} %get-tuple-element.115, bf16[8,768,128]{2,1,0:T(8,128)(2,1)} %get-tuple-element.117, bf16[16,8,32,128]{3,2,1,0:T(8,128)(2,1)} %get-tuple-element.116, s32[]{:T(128)} %get-tuple-element.106), kind=kOutput, calls=%fused_computation.1.clone.1 | convolution fusion | flops 405796864 | bytes 1653248 | tf_op jit(solution)/shard_map/while/body/eval_jaxpr/qtd,psd->qtps/dot_general | solution.py:18
  73.2 2.5 %select_reduce_fusion.2 = f32[8,32,8]{1,2,0:T(8,128)S(1)} fusion(pred[8,768]{1,0:T(8,128)(4,1)S(1)} %get-tuple-element.115, bf16[8,768,128]{2,1,0:T(8,128)(2,1)} %get-tuple-element.117, bf16[16,8,32,128]{3,2,1,0:T(8,128)(2,1)} %get-tuple-element.116, s32[]{:T(128)} %get-tuple-element.106), kind=kOutput, calls=%fused_computation.1.clone.1 | convolution fusion | flops 405796864 | bytes 1653248 | tf_op jit(solution)/shard_map/while/body/eval_jaxpr/qtd,psd->qtps/dot_general | solution.py:18
  75.8 2.5 %select_reduce_fusion.2 = f32[8,32,8]{1,2,0:T(8,128)S(1)} fusion(pred[8,768]{1,0:T(8,128)(4,1)S(1)} %get-tuple-element.115, bf16[8,768,128]{2,1,0:T(8,128)(2,1)} %get-tuple-element.117, bf16[16,8,32,128]{3,2,1,0:T(8,128)(2,1)} %get-tuple-element.116, s32[]{:T(128)} %get-tuple-element.106), kind=kOutput, calls=%fused_computation.1.clone.1 | convolution fusion | flops 405796864 | bytes 1653248 | tf_op jit(solution)/shard_map/while/body/eval_jaxpr/qtd,psd->qtps/dot_general | solution.py:18
  78.4 2.5 %select_reduce_fusion.2 = f32[8,32,8]{1,2,0:T(8,128)S(1)} fusion(pred[8,768]{1,0:T(8,128)(4,1)S(1)} %get-tuple-element.115, bf16[8,768,128]{2,1,0:T(8,128)(2,1)} %get-tuple-element.117, bf16[16,8,32,128]{3,2,1,0:T(8,128)(2,1)} %get-tuple-element.116, s32[]{:T(128)} %get-tuple-element.106), kind=kOutput, calls=%fused_computation.1.clone.1 | convolution fusion | flops 405796864 | bytes 1653248 | tf_op jit(solution)/shard_map/while/body/eval_jaxpr/qtd,psd->qtps/dot_general | solution.py:18
  81.0 2.5 %select_reduce_fusion.2 = f32[8,32,8]{1,2,0:T(8,128)S(1)} fusion(pred[8,768]{1,0:T(8,128)(4,1)S(1)} %get-tuple-element.115, bf16[8,768,128]{2,1,0:T(8,128)(2,1)} %get-tuple-element.117, bf16[16,8,32,128]{3,2,1,0:T(8,128)(2,1)} %get-tuple-element.116, s32[]{:T(128)} %get-tuple-element.106), kind=kOutput, calls=%fused_computation.1.clone.1 | convolution fusion | flops 405796864 | bytes 1653248 | tf_op jit(solution)/shard_map/while/body/eval_jaxpr/qtd,psd->qtps/dot_general | solution.py:18
  83.6 2.5 %select_reduce_fusion.2 = f32[8,32,8]{1,2,0:T(8,128)S(1)} fusion(pred[8,768]{1,0:T(8,128)(4,1)S(1)} %get-tuple-element.115, bf16[8,768,128]{2,1,0:T(8,128)(2,1)} %get-tuple-element.117, bf16[16,8,32,128]{3,2,1,0:T(8,128)(2,1)} %get-tuple-element.116, s32[]{:T(128)} %get-tuple-element.106), kind=kOutput, calls=%fused_computation.1.clone.1 | convolution fusion | flops 405796864 | bytes 1653248 | tf_op jit(solution)/shard_map/while/body/eval_jaxpr/qtd,psd->qtps/dot_general | solution.py:18
  86.2 2.5 %select_reduce_fusion.2 = f32[8,32,8]{1,2,0:T(8,128)S(1)} fusion(pred[8,768]{1,0:T(8,128)(4,1)S(1)} %get-tuple-element.115, bf16[8,768,128]{2,1,0:T(8,128)(2,1)} %get-tuple-element.117, bf16[16,8,32,128]{3,2,1,0:T(8,128)(2,1)} %get-tuple-element.116, s32[]{:T(128)} %get-tuple-element.106), kind=kOutput, calls=%fused_computation.1.clone.1 | convolution fusion | flops 405796864 | bytes 1653248 | tf_op jit(solution)/shard_map/while/body/eval_jaxpr/qtd,psd->qtps/dot_general | solution.py:18
  88.8 2.5 %select_reduce_fusion.2 = f32[8,32,8]{1,2,0:T(8,128)S(1)} fusion(pred[8,768]{1,0:T(8,128)(4,1)S(1)} %get-tuple-element.115, bf16[8,768,128]{2,1,0:T(8,128)(2,1)} %get-tuple-element.117, bf16[16,8,32,128]{3,2,1,0:T(8,128)(2,1)} %get-tuple-element.116, s32[]{:T(128)} %get-tuple-element.106), kind=kOutput, calls=%fused_computation.1.clone.1 | convolution fusion | flops 405796864 | bytes 1653248 | tf_op jit(solution)/shard_map/while/body/eval_jaxpr/qtd,psd->qtps/dot_general | solution.py:18
  91.4 2.5 %select_reduce_fusion.2 = f32[8,32,8]{1,2,0:T(8,128)S(1)} fusion(pred[8,768]{1,0:T(8,128)(4,1)S(1)} %get-tuple-element.115, bf16[8,768,128]{2,1,0:T(8,128)(2,1)} %get-tuple-element.117, bf16[16,8,32,128]{3,2,1,0:T(8,128)(2,1)} %get-tuple-element.116, s32[]{:T(128)} %get-tuple-element.106), kind=kOutput, calls=%fused_computation.1.clone.1 | convolution fusion | flops 405796864 | bytes 1653248 | tf_op jit(solution)/shard_map/while/body/eval_jaxpr/qtd,psd->qtps/dot_general | solution.py:18
  94.2 6.1 %all_to_all.10 = f32[4,1,256]{2,1,0:T(1,128)S(1)} all-to-all(f32[4,1,256]{2,1,0:T(1,128)S(1)} %reshape.50), channel_id=1, replica_groups=mesh['replica'=2,'data2'=4,'data'=4] {'data'}, dimensions={0} | all-to-all | bytes 8192 | tf_op jit(solution)/shard_map/all_to_all | solution.py:49
  102.4 3.5 %all-to-all-start.1 = ((f32[4,1,256]{2,1,0:T(1,128)}), f32[4,1,256]{2,1,0:T(1,128)S(1)}, u32[]{:S(2)}, u32[]{:S(2)}) async-start(f32[4,1,256]{2,1,0:T(1,128)} %reshape.52), calls=%async_computation.1 | async-start | bytes 8192 | tf_op jit(solution)/shard_map/all_to_all | solution.py:50
  106.5 4.7 %all-to-all-done.1 = f32[4,1,256]{2,1,0:T(1,128)S(1)} async-done(((f32[4,1,256]{2,1,0:T(1,128)}), f32[4,1,256]{2,1,0:T(1,128)S(1)}, u32[]{:S(2)}, u32[]{:S(2)}) %all-to-all-start.1) | async-done | bytes 4128 | tf_op jit(solution)/shard_map/all_to_all | solution.py:50
  114.4 30.1 %psum.7 = f32[]{:T(128)} all-reduce(f32[]{:T(128)} %get-tuple-element.60), channel_id=1, replica_groups=mesh['replica'=2,'data2'=4,'data'=4] {'data2','data'}, use_global_device_ids=true, to_apply=%region_9.10 | all-reduce | flops 1 | bytes 8 | tf_op jit(solution)/shard_map/psum | solution.py:54
  (63 shorter events, 12.6 us)
Async XLA Ops:
  7.2 1.2 copy-start
  7.2 45.1 %all-gather.2.cloned.1.call-start = ((), (), s32[]{:S(2)}) async-start(), calls=%async_computation.2 | async-start | bytes 1114112 | tf_op jit(solution)/shard_map/all_gather | solution.py:42
  25.9 3.8 %copy-start.1 = (s32[8,768]{1,0:T(8,128)S(1)}, s32[8,768]{1,0:T(8,128)}, u32[]{:S(2)}) copy-start(s32[8,768]{1,0:T(8,128)} %param.12) | copy-start | bytes 73732
  102.4 8.9 %all-to-all-start.1 = ((f32[4,1,256]{2,1,0:T(1,128)}), f32[4,1,256]{2,1,0:T(1,128)S(1)}, u32[]{:S(2)}, u32[]{:S(2)}) async-start(f32[4,1,256]{2,1,0:T(1,128)} %reshape.52), calls=%async_computation.1 | async-start | bytes 8192 | tf_op jit(solution)/shard_map/all_to_all | solution.py:50
Sparse Core Ops, SparseCore 0:
  11.6 40.6 all-gather.1
where the time goes:
time: 154 us; the launch traced here: 153 us
  matrix products  56.1 us (36%)
  blocking collectives  36.2 us (24%)
  waiting for transfers between devices  27.4 us (18%)
  between operations  16.6 us (11%)
  other arithmetic  7.82 us (5%)
  local copies, waits for them, and re-layouts  5.37 us (3%)
  starting transfers between devices  3.52 us (2%)
    dot_general x16, matrix products, block_scores(): jnp.einsum('qtd,psd->qtps', q_block, d_tok, preferred_element_type=jnp.fl...  40.1 us
    psum x1, blocking collectives, device_fn(): lax.psum(jnp.sum(loss_rows), GROUP_AXES) / (group_size * per_dev)  30.1 us
    all_gather x1, waiting for transfers between devices, device_fn(): all_q = lax.all_gather(q_tok, GROUP_AXES, axis=0, tiled=True)  22.7 us
    dot_general x2, matrix products, project(): jnp.einsum('bld,de->ble', hidden, w_proj, preferred_element_type=jnp.floa...  15.9 us
    all_to_all x1, blocking collectives, device_fn(): col_scores = lax.all_to_all(col_scores, 'data', 1, 1, tiled=True)  6.14 us
    all_to_all x1, waiting for transfers between devices, device_fn(): col_scores = lax.all_to_all(col_scores, 'data2', 0, 0, tiled=True)  4.71 us
    all_to_all x1, starting transfers between devices, device_fn(): col_scores = lax.all_to_all(col_scores, 'data2', 0, 0, tiled=True)  3.48 us
  transfers between devices with their start and end apart: 2, of which 2 were waited for; matrix products, arithmetic and copies ran while one was open for 12% of the time, Pallas kernels for 0%

commit v1 on v0

v1 whole, which is shorter than its diff:
```python
import jax
import jax.numpy as jnp
from jax import lax
from jax.experimental import pallas as pl
from jax.experimental.pallas import tpu as pltpu
from jax.sharding import PartitionSpec as P

NORM_EPS = 1e-6
ROW_AXES = ('replica', 'data2', 'data')
MESH = pl.DeviceIdType.MESH
F32, BF16 = jnp.float32, jnp.bfloat16
MASKED = -1e30

DOCS, DLEN, QLEN, HID, PROJ = 8, 768, 32, 2048, 128
ROWS = DOCS * DLEN
CHUNK = 512
NCHUNK = ROWS // CHUNK
TILE = 256
GROUP = 2
SGROUP = 2
QROWS = DOCS * QLEN
NBLK, NCHIP = 16, 8


def kernel(q_hbm, d_hbm, w_hbm, qm_hbm, dm_hbm, t_hbm, loss_ref, mean_ref,
           x, qh, wv, ext, qall, qf, bias, rs, sall, qm, dm, tv,
           dsem, isem, bsend, brecv, fsend, frecv, ssend, srecv):
    z, d = lax.axis_index('data2'), lax.axis_index('data')
    y, c = d // 2, d % 2
    me = z * 4 + d

    def peer(k):
        ky, k0, k1 = k % 2, (k // 2) % 2, k // 4
        pz = (z % 2 + k0) % 2 + 2 * ((z // 2 + k1) % 2)
        return pz, ((y + ky) % 2) * 2 + c

    def chip_of(k):
        pz, pd = peer(k)
        return pz * 2 + pd // 2

    def send_block(k):
        pz, pd = peer(k)
        return pltpu.make_async_remote_copy(
            src_ref=qall.at[me], dst_ref=qall.at[me], send_sem=bsend.at[k], recv_sem=brecv.at[k],
            device_id={'data2': pz, 'data': pd}, device_id_type=MESH)

    def recv_block(k):
        pz, pd = peer(k)
        blk = pz * 4 + pd
        return pltpu.make_async_remote_copy(
            src_ref=qall.at[blk], dst_ref=qall.at[blk], send_sem=bsend.at[k], recv_sem=brecv.at[k],
            device_id={'data2': pz, 'data': pd}, device_id_type=MESH)

    def forward(k):
        blk = chip_of(k) * 2 + c
        return pltpu.make_async_remote_copy(
            src_ref=qall.at[blk], dst_ref=qall.at[blk], send_sem=fsend.at[k], recv_sem=frecv.at[k],
            device_id={'data2': z, 'data': y * 2 + 1 - c}, device_id_type=MESH)

    def recv_forward(k):
        blk = chip_of(k) * 2 + 1 - c
        return pltpu.make_async_remote_copy(
            src_ref=qall.at[blk], dst_ref=qall.at[blk], send_sem=fsend.at[k], recv_sem=frecv.at[k],
            device_id={'data2': z, 'data': y * 2 + 1 - c}, device_id_type=MESH)

    def any_peer(k):
        pz, pd = peer(k // 2)
        return pz, (pd // 2) * 2 + (c + k % 2) % 2

    def send_scores(k):
        pz, pd = any_peer(k)
        return pltpu.make_async_remote_copy(
            src_ref=sall.at[me], dst_ref=sall.at[me], send_sem=ssend.at[k], recv_sem=srecv.at[k],
            device_id={'data2': pz, 'data': pd}, device_id_type=MESH)

    def recv_scores(k):
        pz, pd = any_peer(k)
        blk = pz * 4 + pd
        return pltpu.make_async_remote_copy(
            src_ref=sall.at[blk], dst_ref=sall.at[blk], send_sem=ssend.at[k], recv_sem=srecv.at[k],
            device_id={'data2': pz, 'data': pd}, device_id_type=MESH)

    def chunk_copy(t):
        return pltpu.make_async_copy(d_hbm.at[pl.ds(pl.multiple_of(t * CHUNK, CHUNK), CHUNK), :], x.at[t], dsem.at[t])

    copies = [pltpu.make_async_copy(a, b, isem.at[i]) for i, (a, b) in enumerate(
        ((w_hbm, wv), (q_hbm, qh), (qm_hbm, qm), (dm_hbm, dm), (t_hbm, tv)))]
    for copy in copies:
        copy.start()
    for t in range(NCHUNK):
        chunk_copy(t).start()

    barrier = pltpu.get_barrier_semaphore()
    for k in range(1, NBLK):
        pz, pd = any_peer(k)
        pl.semaphore_signal(barrier, inc=1, device_id={'data2': pz, 'data': pd}, device_id_type=MESH)

    def unit(proj):
        return proj * lax.rsqrt(jnp.sum(proj * proj, axis=1, keepdims=True) + NORM_EPS)

    def dot(a, b):
        return lax.dot_general(a, b, (((1,), (0,)), ((), ())), preferred_element_type=F32)

    for i in range(3):
        copies[i].wait()
    qf[...] = unit(dot(qh[...], wv[...]))
    rows = []
    for t in range(QLEN):
        keep = qm[:, t:t + 1] > 0
        rows.append(jnp.where(keep, qf[pl.ds(t, DOCS, stride=QLEN), :], 0.0))
    qall[me] = jnp.concatenate(rows, axis=0).astype(BF16)

    copies[3].wait()
    pad = jnp.where(dm[...] > 0, 0.0, MASKED).astype(F32)
    pad = jnp.concatenate([pad, jnp.zeros((120, DLEN), F32)], axis=0)
    for i in range(DLEN // 128):
        bias[pl.ds(i * 128, 128), :] = pad[:, i * 128:(i + 1) * 128].T
    lane = lax.broadcasted_iota(jnp.int32, (TILE, 128), 1)

    def project_chunk(t):
        chunk_copy(t).wait()
        row = pl.multiple_of(t * CHUNK, CHUNK)
        ext[pl.ds(row, CHUNK), 0:128] = unit(dot(x[t], wv[...])).astype(BF16)
        for n in range(CHUNK // TILE):
            tile = t * (CHUNK // TILE) + n
            part = bias[pl.ds(pl.multiple_of((tile % 3) * TILE, TILE), TILE), :]
            ext[pl.ds(row + n * TILE, TILE), 128:256] = jnp.where(lane == tile // 3, part, 0.0).astype(BF16)

    def project_group(i, _):
        for n in range(GROUP):
            project_chunk(i * GROUP + n)
        return 0

    project_group(0, 0)
    pl.semaphore_wait(barrier, NBLK - 1)
    forward(0).start()
    for k in range(1, NCHIP):
        send_block(k).start()
    lax.fori_loop(1, NCHUNK // GROUP - 1, project_group, 0)
    recv_block(1).wait_recv()
    forward(1).start()
    project_group(NCHUNK // GROUP - 1, 0)

    ones_ext = jnp.where(lane < DOCS, 1.0, 0.0).astype(BF16)

    def stage(p, fwd, nxt):
        chip = chip_of(p)
        blocks = [jnp.concatenate([qall[chip * 2 + q], ones_ext], axis=1) for q in (0, 1)]
        for j in range(DOCS):
            if j == DOCS // 2:
                if fwd:
                    recv_block(p + 2).wait_recv()
                    forward(p + 2).start()
                if nxt:
                    recv_forward(p + 1).wait_recv()
            for q in (0, 1):
                sim = lax.dot_general(ext[pl.ds(j * DLEN, DLEN), :], blocks[q], (((1,), (1,)), ((), ())), preferred_element_type=F32)
                best = jnp.max(sim.reshape(DLEN // 8, 8, TILE), axis=0)
                rs[q, pl.ds(chip * DOCS + j, 1), :] = jnp.max(best, axis=0, keepdims=True)

    def stages(i, _):
        for n in range(SGROUP):
            stage(i * SGROUP + n, True, True)
        return 0

    recv_forward(0).wait_recv()
    lax.fori_loop(0, (NCHIP - 2) // SGROUP, stages, 0)
    stage(NCHIP - 2, False, True)
    stage(NCHIP - 1, False, False)

    half = lax.broadcasted_iota(jnp.int32, (DOCS, 128), 1)
    vals = []
    for b in range(NBLK):
        v = rs[b % 2, pl.ds(8 * (b // 2), 8), :]
        vals.append(v[:, :128] + v[:, 128:])
    for width in (64, 32, 16, 8):
        n = len(vals) // 2
        low = (half // width) % 2 == 0
        nxt = []
        for i in range(n):
            keep = jnp.where(low, vals[i], vals[i + n])
            move = jnp.where(low, vals[i + n], vals[i])
            fold = jnp.where(low, pltpu.roll(move, 128 - width, axis=1), pltpu.roll(move, width, axis=1)) if width < 64 else pltpu.roll(move, 64, axis=1)
            nxt.append(keep + fold)
        vals = nxt
    sall[me] = vals[0]

    for k in range(1, NBLK):
        send_scores(k).start()
    copies[4].wait()
    temp = tv[0]
    for k in range(1, NBLK):
        recv_scores(k).wait_recv()
    logits = sall[...] / temp
    top = jnp.max(jnp.max(logits, axis=0), axis=0, keepdims=True)
    total = jnp.sum(jnp.sum(jnp.exp(logits - top[None]), axis=0), axis=0, keepdims=True)
    doc = lax.broadcasted_iota(jnp.int32, (NBLK, DOCS, 128), 0) * DOCS + lax.broadcasted_iota(jnp.int32, (NBLK, DOCS, 128), 1)
    own = doc == lax.broadcasted_iota(jnp.int32, (NBLK, DOCS, 128), 2)
    pos = jnp.sum(jnp.sum(jnp.where(own, logits, 0.0), axis=0), axis=0, keepdims=True)
    loss = top + jnp.log(total) - pos
    mean_ref[...] = jnp.sum(loss, axis=1, keepdims=True) / (NBLK * DOCS)
    loss_ref[...] = pltpu.roll(jnp.broadcast_to(loss, (8, 128)), lax.rem(128 - me * DOCS, 128), axis=1)[0:1, :DOCS]

    for k in range(1, NCHIP):
        send_block(k).wait_send()
    for k in range(NCHIP):
        forward(k).wait_send()
    for k in range(1, NBLK):
        send_scores(k).wait_send()


def solution(mesh):
    def device_fn(q_hidden, d_hidden, w_proj, q_mask, d_mask, temperature):
        hbm = pl.BlockSpec(memory_space=pltpu.HBM)
        vmem = pl.BlockSpec(memory_space=pltpu.VMEM)
        dma = pltpu.SemaphoreType.DMA
        loss, mean = pl.pallas_call(
            kernel,
            out_shape=(jax.ShapeDtypeStruct((1, DOCS), F32), jax.ShapeDtypeStruct((1, 1), F32)),
            in_specs=[hbm] * 6,
            out_specs=(vmem, vmem),
            scratch_shapes=[
                pltpu.VMEM((NCHUNK, CHUNK, HID), BF16),
                pltpu.VMEM((QROWS, HID), BF16),
                pltpu.VMEM((HID, PROJ), BF16),
                pltpu.VMEM((ROWS, 256), BF16),
                pltpu.VMEM((NBLK, QROWS, PROJ), BF16),
                pltpu.VMEM((QROWS, PROJ), F32),
                pltpu.VMEM((DLEN, 128), F32),
                pltpu.VMEM((2, DOCS * NCHIP, 256), F32),
                pltpu.VMEM((NBLK, DOCS, 128), F32),
                pltpu.VMEM((DOCS, QLEN), jnp.int32),
                pltpu.VMEM((DOCS, DLEN), jnp.int32),
                pltpu.SMEM((1,), F32),
                dma((NCHUNK,)), dma((5,)), dma((NCHIP,)), dma((NCHIP,)), dma((NCHIP,)), dma((NCHIP,)), dma((NBLK,)), dma((NBLK,)),
            ],
            compiler_params=pltpu.CompilerParams(collective_id=0, has_side_effects=True, vmem_limit_bytes=60 * 2**20),
            name='late_interaction',
        )(q_hidden.reshape(QROWS, HID), d_hidden.reshape(ROWS, HID), w_proj, q_mask, d_mask, temperature.reshape(1))
        return loss.reshape(DOCS), mean.reshape(1)

    return jax.shard_map(
        device_fn,
        mesh=mesh,
        in_specs=(P(ROW_AXES), P(ROW_AXES), P(), P(ROW_AXES), P(ROW_AXES), P()),
        out_specs=(P(ROW_AXES), P('replica')),
        check_vma=False,
    )
```

time: 154 us -> 53.2 us (0.35)
  matrix products: 56.1 us -> 0 us
  Pallas kernels: 0 us -> 48.9 us
  blocking collectives: 36.2 us -> 0 us
  waiting for transfers between devices: 27.4 us -> 0 us
  between operations: 16.6 us -> 3.05 us
  other arithmetic: 7.82 us -> 0 us
  local copies, waits for them, and re-layouts: 5.37 us -> 1.11 us
  starting transfers between devices: 3.52 us -> 0 us
    dot_general x18 -> x0, matrix products: 56.1 us -> none  [the longest x16 40.1 us: block_scores(): jnp.einsum('qtd,psd->qtps', q_block, d_tok, preferred_element_type=jnp.fl...]
    pallas_call x0 -> x1, Pallas kernels: none -> 48.9 us  [device_fn(): pl.pallas_call(kernel, out_shape=(jax.ShapeDtypeStruct((1, DOCS), F32), j...]
    psum x1 -> x0, blocking collectives: 30.1 us -> none  [device_fn(): lax.psum(jnp.sum(loss_rows), GROUP_AXES) / (group_size * per_dev)]
    all_gather x1 -> x0, waiting for transfers between devices: 22.7 us -> none  [device_fn(): all_q = lax.all_gather(q_tok, GROUP_AXES, axis=0, tiled=True)]
    all_to_all x1 -> x0, blocking collectives: 6.14 us -> none  [device_fn(): col_scores = lax.all_to_all(col_scores, 'data', 1, 1, tiled=True)]
    all_to_all x1 -> x0, waiting for transfers between devices: 4.71 us -> none  [device_fn(): col_scores = lax.all_to_all(col_scores, 'data2', 0, 0, tiled=True)]
    all_to_all x1 -> x0, starting transfers between devices: 3.48 us -> none  [device_fn(): col_scores = lax.all_to_all(col_scores, 'data2', 0, 0, tiled=True)]
    reduce_sum x18 -> x0, other arithmetic: 2.68 us -> none  [the longest x16 1.33 us: block_scores(): return jnp.sum(jnp.max(sim_vals, axis=-1), axis=1)]
  transfers between devices with their start and end apart: 2 -> 0, of which waited for: 2 -> 0; matrix products, arithmetic and copies ran while one was open for 12% -> 0% of each run, Pallas kernels for 0% -> 0%
where the time goes in v1:
time: 53.2 us; the launch traced here: 53 us
  Pallas kernels  48.9 us (92%)
  between operations  3.05 us (6%)
  local copies, waits for them, and re-layouts  1.11 us (2%)
    pallas_call x1, Pallas kernels, device_fn(): pl.pallas_call(kernel, out_shape=(jax.ShapeDtypeStruct((1, DOCS), F32), j...  48.9 us
    unnamed x1, local copies, waits for them, and re-layouts  1.11 us

profile of v1, /device:TPU:0, one launch (start us, length us, event | category | flops | bytes accessed | tf_op | source)
XLA Modules:
  0.0 53.0 jit_solution(16702601592750610857)
XLA Ops:
  1.3 48.9 %late_interaction.1 = (f32[1,8]{1,0:T(1,128)}, f32[1,1]{1,0:T(1,128)}) custom-call(bf16[256,2048]{1,0:T(8,128)(2,1)} %bitcast.7, bf16[6144,2048]{1,0:T(8,128)(2,1)} %bitcast.6, bf16[2048,128]{1,0:T(8,128)(2,1)} %w_hbm.1, s32[8,32]{1,0:T(8,128)} %qm_hbm.1, s32[8,768]{1,0:T(8,128)} %dm_hbm.1, f32[1]{0:T(128)} %bitcast.5.t_hbm), custom_call_target="tpu_custom_call" | custom-call | tf_op jit(solution)/shard_map/late_interaction/pallas_call | solution.py:217
  50.2 1.1 %copy.11 = f32[8]{0:T(128)} copy(f32[8]{0:T(128)} %bitcast.8) | data formatting | bytes 64

commit v2 on v1

--- a/solution.py
+++ b/solution.py
@@ -15,9 +15,11 @@
 ROWS = DOCS * DLEN
 CHUNK = 512
 NCHUNK = ROWS // CHUNK
+AHEAD = 5
+STEP = 1536
+NSTEP = ROWS // STEP
+SGROUP = 1
 TILE = 256
-GROUP = 2
-SGROUP = 2
 QROWS = DOCS * QLEN
 NBLK, NCHIP = 16, 8
 
@@ -81,14 +83,14 @@
             device_id={'data2': pz, 'data': pd}, device_id_type=MESH)
 
     def chunk_copy(t):
-        return pltpu.make_async_copy(d_hbm.at[pl.ds(pl.multiple_of(t * CHUNK, CHUNK), CHUNK), :], x.at[t], dsem.at[t])
+        return pltpu.make_async_copy(d_hbm.at[pl.ds(pl.multiple_of(t * CHUNK, CHUNK), CHUNK), :],
+                                     x.at[pl.ds(pl.multiple_of(t * CHUNK, CHUNK), CHUNK), :], dsem.at[t])
 
     copies = [pltpu.make_async_copy(a, b, isem.at[i]) for i, (a, b) in enumerate(
         ((w_hbm, wv), (q_hbm, qh), (qm_hbm, qm), (dm_hbm, dm), (t_hbm, tv)))]
     for copy in copies:
         copy.start()
-    for t in range(NCHUNK):
-        chunk_copy(t).start()
+    chunk_copy(0).start()
 
     barrier = pltpu.get_barrier_semaphore()
     for k in range(1, NBLK):
@@ -103,6 +105,8 @@
 
     for i in range(3):
         copies[i].wait()
+    for t in range(1, AHEAD):
+        chunk_copy(t).start()
     qf[...] = unit(dot(qh[...], wv[...]))
     rows = []
     for t in range(QLEN):
@@ -117,56 +121,62 @@
         bias[pl.ds(i * 128, 128), :] = pad[:, i * 128:(i + 1) * 128].T
     lane = lax.broadcasted_iota(jnp.int32, (TILE, 128), 1)
 
-    def project_chunk(t):
-        chunk_copy(t).wait()
-        row = pl.multiple_of(t * CHUNK, CHUNK)
-        ext[pl.ds(row, CHUNK), 0:128] = unit(dot(x[t], wv[...])).astype(BF16)
-        for n in range(CHUNK // TILE):
-            tile = t * (CHUNK // TILE) + n
-            part = bias[pl.ds(pl.multiple_of((tile % 3) * TILE, TILE), TILE), :]
-            ext[pl.ds(row + n * TILE, TILE), 128:256] = jnp.where(lane == tile // 3, part, 0.0).astype(BF16)
-
-    def project_group(i, _):
-        for n in range(GROUP):
-            project_chunk(i * GROUP + n)
+    ones_ext = jnp.where(lane < DOCS, 1.0, 0.0).astype(BF16)
+
+    def query_blocks(chip):
+        return [jnp.concatenate([qall[chip * 2 + q], ones_ext], axis=1) for q in (0, 1)]
+
+    def score(blocks, chip, j):
+        docs = ext[pl.ds(pl.multiple_of(j * DLEN, DLEN), DLEN), :]
+        for q in (0, 1):
+            sim = lax.dot_general(docs, blocks[q], (((1,), (1,)), ((), ())), preferred_element_type=F32)
+            best = jnp.max(sim.reshape(DLEN // 8, 8, TILE), axis=0)
+            rs[q, pl.ds(chip * DOCS + j, 1), :] = jnp.max(best, axis=0, keepdims=True)
+
+    def project_step(t, _):
+        for n in range(STEP // CHUNK):
+            chunk = t * (STEP // CHUNK) + n
+            chunk_copy(chunk).wait()
+
+            @pl.when(chunk < NCHUNK - AHEAD)
+            def _():
+                chunk_copy(chunk + AHEAD).start()
+
+        row = pl.multiple_of(t * STEP, STEP)
+        ext[pl.ds(row, STEP), 0:128] = unit(dot(x[pl.ds(row, STEP), :], wv[...])).astype(BF16)
+        for n in range(STEP // TILE):
+            part = bias[pl.ds((n % 3) * TILE, TILE), :]
+            ext[pl.ds(row + n * TILE, TILE), 128:256] = jnp.where(lane == t * 2 + n // 3, part, 0.0).astype(BF16)
         return 0
 
-    project_group(0, 0)
     pl.semaphore_wait(barrier, NBLK - 1)
     forward(0).start()
     for k in range(1, NCHIP):
         send_block(k).start()
-    lax.fori_loop(1, NCHUNK // GROUP - 1, project_group, 0)
-    recv_block(1).wait_recv()
-    forward(1).start()
-    project_group(NCHUNK // GROUP - 1, 0)
-
-    ones_ext = jnp.where(lane < DOCS, 1.0, 0.0).astype(BF16)
-
-    def stage(p, fwd, nxt):
-        chip = chip_of(p)
-        blocks = [jnp.concatenate([qall[chip * 2 + q], ones_ext], axis=1) for q in (0, 1)]
-        for j in range(DOCS):
-            if j == DOCS // 2:
-                if fwd:
-                    recv_block(p + 2).wait_recv()
-                    forward(p + 2).start()
-                if nxt:
-                    recv_forward(p + 1).wait_recv()
-            for q in (0, 1):
-                sim = lax.dot_general(ext[pl.ds(j * DLEN, DLEN), :], blocks[q], (((1,), (1,)), ((), ())), preferred_element_type=F32)
-                best = jnp.max(sim.reshape(DLEN // 8, 8, TILE), axis=0)
-                rs[q, pl.ds(chip * DOCS + j, 1), :] = jnp.max(best, axis=0, keepdims=True)
+    lax.fori_loop(0, NSTEP, project_step, 0)
+
+    for k in range(1, SGROUP):
+        recv_block(k).wait_recv()
+        forward(k).start()
 
     def stages(i, _):
         for n in range(SGROUP):
-            stage(i * SGROUP + n, True, True)
+            recv_forward(i * SGROUP + n).wait_recv()
+
+        @pl.when(i < NCHIP // SGROUP - 1)
+        def _():
+            for n in range(SGROUP):
+                recv_block((i + 1) * SGROUP + n).wait_recv()
+                forward((i + 1) * SGROUP + n).start()
+
+        for n in range(SGROUP):
+            chip = chip_of(i * SGROUP + n)
+            blocks = query_blocks(chip)
+            for j in range(DOCS):
+                score(blocks, chip, j)
         return 0
 
-    recv_forward(0).wait_recv()
-    lax.fori_loop(0, (NCHIP - 2) // SGROUP, stages, 0)
-    stage(NCHIP - 2, False, True)
-    stage(NCHIP - 1, False, False)
+    lax.fori_loop(0, NCHIP // SGROUP, stages, 0)
 
     half = lax.broadcasted_iota(jnp.int32, (DOCS, 128), 1)
     vals = []
@@ -220,7 +230,7 @@
             in_specs=[hbm] * 6,
             out_specs=(vmem, vmem),
             scratch_shapes=[
-                pltpu.VMEM((NCHUNK, CHUNK, HID), BF16),
+                pltpu.VMEM((ROWS, HID), BF16),
                 pltpu.VMEM((QROWS, HID), BF16),
                 pltpu.VMEM((HID, PROJ), BF16),
                 pltpu.VMEM((ROWS, 256), BF16),

time: 53.2 us -> 40.9 us (0.77)
  Pallas kernels: 48.9 us -> 36.6 us
    pallas_call x1, Pallas kernels: 48.9 us -> 36.6 us  [device_fn(): pl.pallas_call(kernel, out_shape=(jax.ShapeDtypeStruct((1, DOCS), F32), j...]
where the time goes in v2:
time: 40.9 us; the launch traced here: 40.8 us
  Pallas kernels  36.6 us (89%)
  between operations  3.05 us (7%)
  local copies, waits for them, and re-layouts  1.11 us (3%)
    pallas_call x1, Pallas kernels, device_fn(): pl.pallas_call(kernel, out_shape=(jax.ShapeDtypeStruct((1, DOCS), F32), j...  36.6 us
    unnamed x1, local copies, waits for them, and re-layouts  1.11 us

profile of v2, /device:TPU:0, one launch (start us, length us, event | category | flops | bytes accessed | tf_op | source)
XLA Modules:
  0.0 40.8 jit_solution(17437523682039812697)
XLA Ops:
  1.3 36.6 %late_interaction.1 = (f32[1,8]{1,0:T(1,128)}, f32[1,1]{1,0:T(1,128)}) custom-call(bf16[256,2048]{1,0:T(8,128)(2,1)} %bitcast.7, bf16[6144,2048]{1,0:T(8,128)(2,1)} %bitcast.6, bf16[2048,128]{1,0:T(8,128)(2,1)} %w_hbm.1, s32[8,32]{1,0:T(8,128)} %qm_hbm.1, s32[8,768]{1,0:T(8,128)} %dm_hbm.1, f32[1]{0:T(128)} %bitcast.5.t_hbm), custom_call_target="tpu_custom_call" | custom-call | tf_op jit(solution)/shard_map/late_interaction/pallas_call | solution.py:227
  37.9 1.1 %copy.11 = f32[8]{0:T(128)} copy(f32[8]{0:T(128)} %bitcast.8) | data formatting | bytes 64

commit v3 on v2

--- a/solution.py
+++ b/solution.py
@@ -18,14 +18,14 @@
 AHEAD = 5
 STEP = 1536
 NSTEP = ROWS // STEP
-SGROUP = 1
+SGROUP = 2
 TILE = 256
 QROWS = DOCS * QLEN
 NBLK, NCHIP = 16, 8
 
 
-def kernel(q_hbm, d_hbm, w_hbm, qm_hbm, dm_hbm, t_hbm, loss_ref, mean_ref,
-           x, qh, wv, ext, qall, qf, bias, rs, sall, qm, dm, tv,
+def kernel(q_hbm, d_hbm, w_hbm, qm_hbm, dm_hbm, out_ref,
+           x, qh, wv, ext, qall, qf, bias, rs, sall, qm, dm,
            dsem, isem, bsend, brecv, fsend, frecv, ssend, srecv):
     z, d = lax.axis_index('data2'), lax.axis_index('data')
     y, c = d // 2, d % 2
@@ -87,7 +87,7 @@
                                      x.at[pl.ds(pl.multiple_of(t * CHUNK, CHUNK), CHUNK), :], dsem.at[t])
 
     copies = [pltpu.make_async_copy(a, b, isem.at[i]) for i, (a, b) in enumerate(
-        ((w_hbm, wv), (q_hbm, qh), (qm_hbm, qm), (dm_hbm, dm), (t_hbm, tv)))]
+        ((w_hbm, wv), (q_hbm, qh), (qm_hbm, qm), (dm_hbm, dm)))]
     for copy in copies:
         copy.start()
     chunk_copy(0).start()
@@ -142,6 +142,12 @@
             def _():
                 chunk_copy(chunk + AHEAD).start()
 
+        @pl.when(t == NSTEP - 1)
+        def _():
+            for k in range(1, SGROUP):
+                recv_block(k).wait_recv()
+                forward(k).start()
+
         row = pl.multiple_of(t * STEP, STEP)
         ext[pl.ds(row, STEP), 0:128] = unit(dot(x[pl.ds(row, STEP), :], wv[...])).astype(BF16)
         for n in range(STEP // TILE):
@@ -154,10 +160,6 @@
     for k in range(1, NCHIP):
         send_block(k).start()
     lax.fori_loop(0, NSTEP, project_step, 0)
-
-    for k in range(1, SGROUP):
-        recv_block(k).wait_recv()
-        forward(k).start()
 
     def stages(i, _):
         for n in range(SGROUP):
@@ -197,11 +199,21 @@
 
     for k in range(1, NBLK):
         send_scores(k).start()
-    copies[4].wait()
-    temp = tv[0]
     for k in range(1, NBLK):
         recv_scores(k).wait_recv()
-    logits = sall[...] / temp
+    out_ref[...] = sall[...]
+
+    for k in range(1, NCHIP):
+        send_block(k).wait_send()
+    for k in range(NCHIP):
+        forward(k).wait_send()
+    for k in range(1, NBLK):
+        send_scores(k).wait_send()
+
+
+def loss_kernel(s_ref, t_ref, loss_ref, mean_ref):
+    me = lax.axis_index('data2') * 4 + lax.axis_index('data')
+    logits = s_ref[...] / t_ref[0]
     top = jnp.max(jnp.max(logits, axis=0), axis=0, keepdims=True)
     total = jnp.sum(jnp.sum(jnp.exp(logits - top[None]), axis=0), axis=0, keepdims=True)
     doc = lax.broadcasted_iota(jnp.int32, (NBLK, DOCS, 128), 0) * DOCS + lax.broadcasted_iota(jnp.int32, (NBLK, DOCS, 128), 1)
@@ -211,24 +223,17 @@
     mean_ref[...] = jnp.sum(loss, axis=1, keepdims=True) / (NBLK * DOCS)
     loss_ref[...] = pltpu.roll(jnp.broadcast_to(loss, (8, 128)), lax.rem(128 - me * DOCS, 128), axis=1)[0:1, :DOCS]
 
-    for k in range(1, NCHIP):
-        send_block(k).wait_send()
-    for k in range(NCHIP):
-        forward(k).wait_send()
-    for k in range(1, NBLK):
-        send_scores(k).wait_send()
-
 
 def solution(mesh):
     def device_fn(q_hidden, d_hidden, w_proj, q_mask, d_mask, temperature):
         hbm = pl.BlockSpec(memory_space=pltpu.HBM)
         vmem = pl.BlockSpec(memory_space=pltpu.VMEM)
         dma = pltpu.SemaphoreType.DMA
-        loss, mean = pl.pallas_call(
+        scores = pl.pallas_call(
             kernel,
-            out_shape=(jax.ShapeDtypeStruct((1, DOCS), F32), jax.ShapeDtypeStruct((1, 1), F32)),
-            in_specs=[hbm] * 6,
-            out_specs=(vmem, vmem),
+            out_shape=jax.ShapeDtypeStruct((NBLK, DOCS, 128), F32),
+            in_specs=[hbm] * 5,
+            out_specs=vmem,
             scratch_shapes=[
                 pltpu.VMEM((ROWS, HID), BF16),
                 pltpu.VMEM((QROWS, HID), BF16),
@@ -241,12 +246,18 @@
                 pltpu.VMEM((NBLK, DOCS, 128), F32),
                 pltpu.VMEM((DOCS, QLEN), jnp.int32),
                 pltpu.VMEM((DOCS, DLEN), jnp.int32),
-                pltpu.SMEM((1,), F32),
-                dma((NCHUNK,)), dma((5,)), dma((NCHIP,)), dma((NCHIP,)), dma((NCHIP,)), dma((NCHIP,)), dma((NBLK,)), dma((NBLK,)),
+                dma((NCHUNK,)), dma((4,)), dma((NCHIP,)), dma((NCHIP,)), dma((NCHIP,)), dma((NCHIP,)), dma((NBLK,)), dma((NBLK,)),
             ],
             compiler_params=pltpu.CompilerParams(collective_id=0, has_side_effects=True, vmem_limit_bytes=60 * 2**20),
             name='late_interaction',
-        )(q_hidden.reshape(QROWS, HID), d_hidden.reshape(ROWS, HID), w_proj, q_mask, d_mask, temperature.reshape(1))
+        )(q_hidden.reshape(QROWS, HID), d_hidden.reshape(ROWS, HID), w_proj, q_mask, d_mask)
+        loss, mean = pl.pallas_call(
+            loss_kernel,
+            out_shape=(jax.ShapeDtypeStruct((1, DOCS), F32), jax.ShapeDtypeStruct((1, 1), F32)),
+            in_specs=[vmem, pl.BlockSpec(memory_space=pltpu.SMEM)],
+            out_specs=(vmem, vmem),
+            name='loss',
+        )(scores, temperature.reshape(1))
         return loss.reshape(DOCS), mean.reshape(1)
 
     return jax.shard_map(

time: 40.9 us -> 38.7 us (0.946)
  between operations: 3.05 us -> 1.29 us
  local copies, waits for them, and re-layouts: 1.11 us -> 0 us
  Pallas kernels: 36.6 us -> 37.2 us
    unnamed x1 -> x0, local copies, waits for them, and re-layouts: 1.11 us -> none
    pallas_call x1 -> x2, Pallas kernels: 36.6 us -> 37.2 us  [the longest x1 35.7 us: device_fn(): pl.pallas_call(kernel, out_shape=jax.ShapeDtypeStruct((NBLK, DOCS, 128),...]
where the time goes in v3:
time: 38.7 us; the launch traced here: 38.5 us
  Pallas kernels  37.2 us (96%)
  between operations  1.29 us (3%)
    pallas_call x1, Pallas kernels, device_fn(): pl.pallas_call(kernel, out_shape=jax.ShapeDtypeStruct((NBLK, DOCS, 128),...  35.7 us
    pallas_call x1, Pallas kernels, device_fn(): pl.pallas_call(loss_kernel, out_shape=(jax.ShapeDtypeStruct((1, DOCS), F3...  1.49 us

profile of v3, /device:TPU:0, one launch (start us, length us, event | category | flops | bytes accessed | tf_op | source)
XLA Modules:
  0.0 38.5 jit_solution(16804771729122104935)
XLA Ops:
  1.3 35.7 %late_interaction.1.s_ref = f32[16,8,128]{2,1,0:T(8,128)} custom-call(bf16[256,2048]{1,0:T(8,128)(2,1)} %bitcast.7, bf16[6144,2048]{1,0:T(8,128)(2,1)} %bitcast.6, bf16[2048,128]{1,0:T(8,128)(2,1)} %w_hbm.1, s32[8,32]{1,0:T(8,128)} %qm_hbm.1, s32[8,768]{1,0:T(8,128)} %dm_hbm.1), custom_call_target="tpu_custom_call" | custom-call | tf_op jit(solution)/shard_map/late_interaction/pallas_call | solution.py:232
  37.0 1.5 %loss.1 = (f32[1,8]{1,0:T(1,128)}, f32[1,1]{1,0:T(1,128)}) custom-call(f32[16,8,128]{2,1,0:T(8,128)} %late_interaction.1.s_ref, f32[1]{0:T(128)} %bitcast.5.t_ref), custom_call_target="tpu_custom_call" | custom-call | tf_op jit(solution)/shard_map/loss/pallas_call | solution.py:254

commit v4 on v3

--- a/solution.py
+++ b/solution.py
@@ -13,10 +13,11 @@
 
 DOCS, DLEN, QLEN, HID, PROJ = 8, 768, 32, 2048, 128
 ROWS = DOCS * DLEN
-CHUNK = 512
+CHUNK = 768
 NCHUNK = ROWS // CHUNK
-AHEAD = 5
-STEP = 1536
+FIRST = 2
+AHEAD = 4
+STEP = 768
 NSTEP = ROWS // STEP
 SGROUP = 2
 TILE = 256
@@ -90,7 +91,8 @@
         ((w_hbm, wv), (q_hbm, qh), (qm_hbm, qm), (dm_hbm, dm)))]
     for copy in copies:
         copy.start()
-    chunk_copy(0).start()
+    for t in range(FIRST):
+        chunk_copy(t).start()
 
     barrier = pltpu.get_barrier_semaphore()
     for k in range(1, NBLK):
@@ -105,7 +107,7 @@
 
     for i in range(3):
         copies[i].wait()
-    for t in range(1, AHEAD):
+    for t in range(FIRST, AHEAD):
         chunk_copy(t).start()
     qf[...] = unit(dot(qh[...], wv[...]))
     rows = []
@@ -152,7 +154,7 @@
         ext[pl.ds(row, STEP), 0:128] = unit(dot(x[pl.ds(row, STEP), :], wv[...])).astype(BF16)
         for n in range(STEP // TILE):
             part = bias[pl.ds((n % 3) * TILE, TILE), :]
-            ext[pl.ds(row + n * TILE, TILE), 128:256] = jnp.where(lane == t * 2 + n // 3, part, 0.0).astype(BF16)
+            ext[pl.ds(row + n * TILE, TILE), 128:256] = jnp.where(lane == t * (STEP // DLEN) + n // 3, part, 0.0).astype(BF16)
         return 0
 
     pl.semaphore_wait(barrier, NBLK - 1)
@@ -231,7 +233,7 @@
         dma = pltpu.SemaphoreType.DMA
         scores = pl.pallas_call(
             kernel,
-            out_shape=jax.ShapeDtypeStruct((NBLK, DOCS, 128), F32),
+            out_shape=pltpu.VMEM((NBLK, DOCS, 128), F32),
             in_specs=[hbm] * 5,
             out_specs=vmem,
             scratch_shapes=[
@@ -257,7 +259,7 @@
             in_specs=[vmem, pl.BlockSpec(memory_space=pltpu.SMEM)],
             out_specs=(vmem, vmem),
             name='loss',
-        )(scores, temperature.reshape(1))
+        )(pltpu.with_memory_space_constraint(scores, pltpu.VMEM), temperature.reshape(1))
         return loss.reshape(DOCS), mean.reshape(1)
 
     return jax.shard_map(

time: 38.7 us -> 36.8 us (0.951)
  Pallas kernels: 37.2 us -> 35.4 us
    pallas_call x1, Pallas kernels: 35.7 us -> 34.7 us  [device_fn(): pl.pallas_call(kernel, out_shape=pltpu.VMEM((NBLK, DOCS, 128), F32), in_s...]
    pallas_call x1, Pallas kernels: 1.49 us -> 0.65 us  [device_fn(): pl.pallas_call(loss_kernel, out_shape=(jax.ShapeDtypeStruct((1, DOCS), F3...]
where the time goes in v4:
time: 36.8 us; the launch traced here: 36.6 us
  Pallas kernels  35.4 us (96%)
  between operations  1.29 us (4%)
    pallas_call x1, Pallas kernels, device_fn(): pl.pallas_call(kernel, out_shape=pltpu.VMEM((NBLK, DOCS, 128), F32), in_s...  34.7 us

profile of v4, /device:TPU:0, one launch (start us, length us, event | category | flops | bytes accessed | tf_op | source)
XLA Modules:
  0.0 36.6 jit_solution(6523410545945708205)
XLA Ops:
  1.3 34.7 %late_interaction.1.s_ref = f32[16,8,128]{2,1,0:T(8,128)S(1)} custom-call(bf16[256,2048]{1,0:T(8,128)(2,1)} %bitcast.7, bf16[6144,2048]{1,0:T(8,128)(2,1)} %bitcast.6, bf16[2048,128]{1,0:T(8,128)(2,1)} %w_hbm.1, s32[8,32]{1,0:T(8,128)} %qm_hbm.1, s32[8,768]{1,0:T(8,128)} %dm_hbm.1), custom_call_target="tpu_custom_call" | custom-call | tf_op jit(solution)/shard_map/late_interaction/pallas_call | solution.py:234
  36.0 0.7 %loss.1 = (f32[1,8]{1,0:T(1,128)}, f32[1,1]{1,0:T(1,128)}) custom-call(f32[16,8,128]{2,1,0:T(8,128)S(1)} %late_interaction.1.s_ref, f32[1]{0:T(128)} %bitcast.5.t_ref), custom_call_target="tpu_custom_call" | custom-call | tf_op jit(solution)/shard_map/loss/pallas_call | solution.py:256

commit v5 on v4

--- a/solution.py
+++ b/solution.py
@@ -95,7 +95,7 @@
         chunk_copy(t).start()
 
     barrier = pltpu.get_barrier_semaphore()
-    for k in range(1, NBLK):
+    for k in range(NBLK - 1, 0, -1):
         pz, pd = any_peer(k)
         pl.semaphore_signal(barrier, inc=1, device_id={'data2': pz, 'data': pd}, device_id_type=MESH)
 
@@ -199,7 +199,7 @@
         vals = nxt
     sall[me] = vals[0]
 
-    for k in range(1, NBLK):
+    for k in range(NBLK - 1, 0, -1):
         send_scores(k).start()
     for k in range(1, NBLK):
         recv_scores(k).wait_recv()

time: 36.8 us -> 36.4 us (0.989)
  Pallas kernels: 35.4 us -> 35 us
    pallas_call x1, Pallas kernels: 34.7 us -> 34.3 us  [device_fn(): pl.pallas_call(kernel, out_shape=pltpu.VMEM((NBLK, DOCS, 128), F32), in_s...]
where the time goes in v5:
time: 36.4 us; the launch traced here: 36.2 us
  Pallas kernels  35 us (96%)
  between operations  1.29 us (4%)
    pallas_call x1, Pallas kernels, device_fn(): pl.pallas_call(kernel, out_shape=pltpu.VMEM((NBLK, DOCS, 128), F32), in_s...  34.3 us

profile of v5, /device:TPU:0, one launch (start us, length us, event | category | flops | bytes accessed | tf_op | source)
XLA Modules:
  0.0 36.2 jit_solution(7983846245696147341)
XLA Ops:
  1.3 34.3 %late_interaction.1.s_ref = f32[16,8,128]{2,1,0:T(8,128)S(1)} custom-call(bf16[256,2048]{1,0:T(8,128)(2,1)} %bitcast.7, bf16[6144,2048]{1,0:T(8,128)(2,1)} %bitcast.6, bf16[2048,128]{1,0:T(8,128)(2,1)} %w_hbm.1, s32[8,32]{1,0:T(8,128)} %qm_hbm.1, s32[8,768]{1,0:T(8,128)} %dm_hbm.1), custom_call_target="tpu_custom_call" | custom-call | tf_op jit(solution)/shard_map/late_interaction/pallas_call | solution.py:234
  35.6 0.7 %loss.1 = (f32[1,8]{1,0:T(1,128)}, f32[1,1]{1,0:T(1,128)}) custom-call(f32[16,8,128]{2,1,0:T(8,128)S(1)} %late_interaction.1.s_ref, f32[1]{0:T(128)} %bitcast.5.t_ref), custom_call_target="tpu_custom_call" | custom-call | tf_op jit(solution)/shard_map/loss/pallas_call | solution.py:256

commit v6 on v5

--- a/solution.py
+++ b/solution.py
@@ -201,16 +201,15 @@
 
     for k in range(NBLK - 1, 0, -1):
         send_scores(k).start()
-    for k in range(1, NBLK):
-        recv_scores(k).wait_recv()
-    out_ref[...] = sall[...]
-
     for k in range(1, NCHIP):
         send_block(k).wait_send()
     for k in range(NCHIP):
         forward(k).wait_send()
     for k in range(1, NBLK):
         send_scores(k).wait_send()
+    for k in range(1, NBLK):
+        recv_scores(k).wait_recv()
+    out_ref[...] = sall[...]
 
 
 def loss_kernel(s_ref, t_ref, loss_ref, mean_ref):

time: 36.4 us -> 36.3 us (level)
  no operation moved by 1% of the time
where the time goes in v6:
time: 36.3 us; the launch traced here: 36.2 us
  Pallas kernels  34.9 us (96%)
  between operations  1.29 us (4%)
    pallas_call x1, Pallas kernels, device_fn(): pl.pallas_call(kernel, out_shape=pltpu.VMEM((NBLK, DOCS, 128), F32), in_s...  34.3 us

profile of v6, /device:TPU:0, one launch (start us, length us, event | category | flops | bytes accessed | tf_op | source)
XLA Modules:
  0.0 36.2 jit_solution(17670363499714054117)
XLA Ops:
  1.3 34.3 %late_interaction.1.s_ref = f32[16,8,128]{2,1,0:T(8,128)S(1)} custom-call(bf16[256,2048]{1,0:T(8,128)(2,1)} %bitcast.7, bf16[6144,2048]{1,0:T(8,128)(2,1)} %bitcast.6, bf16[2048,128]{1,0:T(8,128)(2,1)} %w_hbm.1, s32[8,32]{1,0:T(8,128)} %qm_hbm.1, s32[8,768]{1,0:T(8,128)} %dm_hbm.1), custom_call_target="tpu_custom_call" | custom-call | tf_op jit(solution)/shard_map/late_interaction/pallas_call | solution.py:233
  35.5 0.7 %loss.1 = (f32[1,8]{1,0:T(1,128)}, f32[1,1]{1,0:T(1,128)}) custom-call(f32[16,8,128]{2,1,0:T(8,128)S(1)} %late_interaction.1.s_ref, f32[1]{0:T(128)} %bitcast.5.t_ref), custom_call_target="tpu_custom_call" | custom-call | tf_op jit(solution)/shard_map/loss/pallas_call | solution.py:255
